TPU v7x, 256 devices: a whole 4x4x8 slice. The times are simulated.
256 devices in a mesh: dp: 4 (over x), vocab: 64 (over z, y, core).
Axes of the slice: x: 4, y: 4, z: 8, core: 2. Of those that a mesh axis runs over, the one named last changes fastest.
Arguments:
- prefill_hidden: bfloat16 [1024, 7168], P(('dp', 'vocab')), may hold values from -60 to 60
- decode_hidden: bfloat16 [256, 7168], P(('dp', 'vocab')), may hold values from -60 to 60
- lm_head: bfloat16 [7168, 129280], P('dp', 'vocab'), as said below
- prefill_targets: int32 [1024], P(('dp', 'vocab')), may hold values from 0 to 129279
- decode_targets: int32 [256], P(('dp', 'vocab')), may hold values from 0 to 129279
- decode_live: int32 [4], P('dp'), may hold values from 1 to 64
Outputs:
- prefill_logprob: float32 [1024], P(('dp', 'vocab'))
- decode_logprob: float32 [256], P(('dp', 'vocab'))
Inputs may be any that keep to these rules, and one draw needn't show every extreme that they name: `lm_head`: entries of order one over the square root of 7168.
All inputs are finite; a program needn't handle non-finite values.
Results may differ from a plain program's by a relative error of at most 0.0003.
Values may be sent and summed in bfloat16 or wider, within the bound.
A program may use at most 128 MiB of HBM per device.

v0:
```python
import jax
import jax.numpy as jnp
from jax import lax
from jax.sharding import Mesh
from jax.sharding import PartitionSpec as P

VOCAB = ("vocab_0", "vocab_1", "vocab_2")
DP_VOCAB = ("dp", "vocab_0", "vocab_1", "vocab_2")


def gathered_once(value, axis):
    leaves = jax.tree.leaves(value)
    sequence = sorted(range(len(leaves)), key=lambda k: -leaves[k].size)
    width = (1, *leaves[sequence[0]].shape)[-1]
    lines = [
        jnp.pad(leaves[k].reshape(-1), (0, -leaves[k].size % width)).reshape(-1, width)
        for k in sequence
    ]
    both, at, found = (lax.all_gather(jnp.concatenate(lines), axis), 0, {})
    for k, line in zip(sequence, lines):
        slab = both[:, at : at + len(line)].reshape(len(both), -1)
        found[k] = slab[:, : leaves[k].size].reshape(-1, *leaves[k].shape)
        at += len(line)
    numbers = iter(range(len(leaves)))
    return jax.tree.map(lambda _: found[next(numbers)], value)


def joined_all(value, axes, combine):
    for axis in axes:
        pieces = gathered_once(value, axis)
        value = jax.tree.map(lambda part: part[0], pieces)
        for k in range(1, lax.axis_size(axis)):
            value = combine(value, jax.tree.map(lambda part: part[k], pieces))
    return value


def softmax_join(left, right):
    new_top = jnp.maximum(left[0], right[0])
    totals = left[1] * jnp.exp(left[0] - new_top) + right[1] * jnp.exp(right[0] - new_top)
    return (new_top, totals, left[2] + right[2])


def body(prefill_hidden, decode_hidden, lm_head, prefill_targets, decode_targets, decode_live):
    pre_rows = prefill_hidden.shape[0]
    dec_rows = decode_hidden.shape[0]
    own_count = pre_rows + dec_rows
    hidden = jnp.concatenate([prefill_hidden, decode_hidden], axis=0)
    targets = jnp.concatenate([prefill_targets, decode_targets], axis=0)
    shard_vocab = lm_head.shape[1]
    vocab_offset = lax.axis_index(VOCAB) * shard_vocab
    group_hidden, group_targets = (
        lax.all_gather(hidden, VOCAB, axis=0, tiled=True),
        lax.all_gather(targets, VOCAB, axis=0, tiled=True),
    )
    every_rows = lax.all_to_all(group_hidden, "dp", split_axis=1, concat_axis=0, tiled=True)
    logits = lax.psum_scatter(
        jnp.dot(every_rows, lm_head, preferred_element_type=jnp.float32),
        "dp",
        scatter_dimension=0,
        tiled=True,
    )
    local_top = jnp.max(logits, axis=1)
    target_hit = (group_targets - vocab_offset)[:, None] == jnp.arange(
        shard_vocab, dtype=jnp.int32
    )[None, :]
    local_picked = jnp.sum(jnp.where(target_hit, logits, jnp.float32(0.0)), axis=1)
    own_start = lax.axis_index(VOCAB) * own_count
    local_total = jnp.sum(jnp.exp(logits - local_top[:, None]), axis=1)
    row_top, totals, picked = joined_all(
        (local_top, local_total, local_picked), VOCAB, softmax_join
    )
    group_values = picked - (row_top + jnp.log(totals))
    own_values = lax.dynamic_slice_in_dim(group_values, own_start, own_count, 0)
    prefill_logprob = own_values[:pre_rows]
    positions = lax.axis_index(VOCAB) * dec_rows + jnp.arange(dec_rows, dtype=jnp.int32)
    decode_logprob = jnp.where(positions < decode_live[0], own_values[pre_rows:], jnp.float32(0.0))
    return (prefill_logprob, decode_logprob)


def solution(mesh):
    split = Mesh(
        mesh.devices.reshape(mesh.shape["dp"], 8, 4, 2), ("dp", "vocab_0", "vocab_1", "vocab_2")
    )
    placed = (
        P(DP_VOCAB, None),
        P(DP_VOCAB, None),
        P("dp", VOCAB),
        P(DP_VOCAB),
        P(DP_VOCAB),
        P("dp"),
    )
    return jax.shard_map(
        body, mesh=split, in_specs=placed, out_specs=(P(DP_VOCAB), P(DP_VOCAB)), check_vma=False
    )
```

profile of v0, /device:TPU:1, one launch (start us, length us, event | category | flops | bytes accessed | tf_op | source)
XLA Modules:
  0.0 330.9 jit_solution(16008943737655418088)
XLA Ops:
  7.2 0.0 all-gather.9.cloned.1.call-start
  7.2 1.5 maximum_bitcast_fusion
  8.8 0.0 all-gather.9.cloned.1.call-update
  8.8 0.0 reduce-scatter.2.cloned.1.call-start
  8.8 87.9 %all-gather.9.cloned.1.call-done = bf16[64,5,7168]{2,1,0:T(8,128)(2,1)} async-done(((bf16[1,5,7168]{2,1,0:T(8,128)(2,1)}), bf16[64,5,7168]{2,1,0:T(8,128)(2,1)}) %all-gather.9.cloned.1.call-update) | async-done | bytes 4587536 | tf_op jit(solution)/shard_map/all_gather | solution.py:52
  96.7 11.4 %all_to_all.14 = bf16[320,4,1792]{2,1,0:T(4,128)(2,1)} reshape(bf16[64,5,7168]{2,1,0:T(8,128)(2,1)} %all-gather.9.cloned.1.call-done) | data formatting | bytes 9175040 | tf_op jit(solution)/shard_map/all_to_all | solution.py:55
  108.1 0.0 slice-start
  108.1 3.0 copy.9
  111.1 0.0 slice-start.1
  111.2 56.6 %all_to_all.19 = bf16[320,4,1792]{2,0,1:T(8,128)(2,1)S(1)} all-to-all(bf16[320,4,1792]{2,0,1:T(8,128)(2,1)S(1)} %copy.9), channel_id=1, replica_groups=mesh['dp'=4,'vocab_0'=8,'vocab_1'=4,'vocab_2'=2] {'dp'}, dimensions={1} | all-to-all | bytes 9175040 | tf_op jit(solution)/shard_map/all_to_all | solution.py:55
  167.8 0.0 slice-done
  167.8 0.0 slice-done.1
  167.8 12.4 %fusion.47 = f32[1280,2020]{1,0:T(8,128)} fusion(bf16[1280,1792]{1,0:T(8,128)(2,1)S(1)} %bitcast.248, bf16[1792,2020]{0,1:T(8,128)(2,1)S(1)} %bitcast.250), kind=kOutput, calls=%fused_computation.95 | convolution fusion | flops 9266790400 | bytes 22169600 | tf_op jit(solution)/shard_map/dot_general | solution.py:57
  180.2 0.0 copy-start.1
  180.2 0.0 copy-start
  180.2 0.0 reduce-scatter.2.cloned.1.call-update
  181.5 0.0 copy-done.1
  181.5 0.6 dynamic-slice
  182.8 0.0 copy-done
  182.8 0.2 add_dynamic-update-slice_fusion
  183.0 15.0 %all-reduce = s32[320]{0:T(512)S(1)} all-reduce(s32[320]{0:T(512)S(1)} %add_dynamic-update-slice_fusion), channel_id=1, replica_groups=mesh['dp'=4,'vocab_0'=8,'vocab_1'=4,'vocab_2'=2] {'vocab_0','vocab_1','v..., use_global_device_ids=true, to_apply=%add | all-reduce | flops 320 | bytes 2560
  198.0 78.1 %reduce-scatter.2.cloned.1.call-done = f32[320,2020]{1,0:T(8,128)} async-done(((f32[1280,2020]{1,0:T(8,128)}), f32[320,2020]{1,0:T(8,128)}) %reduce-scatter.2.cloned.1.call-update) | async-done | bytes 2585616 | tf_op jit(solution)/shard_map/reduce_scatter | solution.py:56
  276.1 2.0 reduce_max.9
  278.0 2.5 exponential_reduce_fusion
  280.6 20.2 %all-gather.4 = f32[8,3,320]{2,1,0:T(4,128)S(1)} all-gather(f32[1,3,320]{2,1,0:T(4,128)S(1)} %maximum_bitcast_fusion.1), channel_id=2, replica_groups=mesh['dp'=4,'vocab_0'=8,'vocab_1'=4,'vocab_2'=2] {'vocab_0'}, dimensions={0}, use_global_device_ids=true | all-gather | bytes 34560 | tf_op jit(solution)/shard_map/all_gather | solution.py:19
  300.9 9.4 %all-gather.5 = f32[4,3,320]{2,1,0:T(4,128)S(1)} all-gather(f32[1,3,320]{2,1,0:T(4,128)S(1)} %maximum_bitcast_fusion.2), channel_id=3, replica_groups=mesh['dp'=4,'vocab_0'=8,'vocab_1'=4,'vocab_2'=2] {'vocab_1'}, dimensions={0}, use_global_device_ids=true | all-gather | bytes 19200 | tf_op jit(solution)/shard_map/all_gather | solution.py:19
  310.4 11.2 %all-gather.6 = f32[2,3,320]{2,1,0:T(4,128)S(1)} all-gather(f32[1,3,320]{2,1,0:T(4,128)S(1)} %maximum_bitcast_fusion.3), channel_id=4, replica_groups=mesh['dp'=4,'vocab_0'=8,'vocab_1'=4,'vocab_2'=2] {'vocab_2'}, dimensions={0}, use_global_device_ids=true | all-gather | bytes 11520 | tf_op jit(solution)/shard_map/all_gather | solution.py:19
  321.6 0.1 dynamic_slice.3
  321.7 0.0 copy-start.2
  321.7 0.6 slice.268
  322.9 0.0 copy-done.2
  (15 shorter events, 0.2 us)
Async XLA Ops:
  7.2 89.5 %all-gather.9.cloned.1.call-start = ((), (), s32[]{:S(2)}) async-start(), calls=%async_computation.3 | async-start | bytes 7454720 | tf_op jit(solution)/shard_map/all_gather | solution.py:52
  8.8 267.3 %reduce-scatter.2.cloned.1.call-start = ((), (), s32[]{:S(2)}) async-start(), calls=%async_computation.2 | async-start | bytes 13107200 | tf_op jit(solution)/shard_map/reduce_scatter | solution.py:56
  108.1 59.6 %slice-start = ((s8[7254016]{0:T(1024)(128)(4,1)}), s8[4194304]{0:T(1024)(128)(4,1)S(1)}, s32[]{:S(2)}) async-start(s8[7254016]{0:T(1024)(128)(4,1)} %bitcast.249), calls=%async_computation.4 | async-start | bytes 8388608
  111.1 56.6 %slice-start.1 = ((s8[7254016]{0:T(1024)(128)(4,1)}), s8[3059712]{0:T(1024)(128)(4,1)S(1)}, s32[]{:S(2)}) async-start(s8[7254016]{0:T(1024)(128)(4,1)} %bitcast.249), calls=%async_computation.5 | async-start | bytes 6119424
  180.2 1.3 copy-start.1
  180.2 2.6 copy-start
  321.7 1.2 copy-start.2
Sparse Core Ops, SparseCore 0:
  10.7 85.9 all-gather.8
  180.3 95.6 reduce-scatter.1
where the time goes:
time: 331 us
  waiting for transfers between devices  166 us (50%)
  blocking collectives  112 us (34%)
  between operations  17.9 us (5%)
  local copies, waits for them, and re-layouts  15.7 us (5%)
  matrix products  12.4 us (4%)
  other arithmetic  6.4 us (2%)
    all_gather x1, waiting for transfers between devices, body(): lax.all_gather(hidden, VOCAB, axis=0, tiled=True)  87.9 us
    reduce_scatter x1, waiting for transfers between devices, body(): lax.psum_scatter(jnp.dot(every_rows, lm_head, preferred_element_type=jnp....  78.1 us
    all_to_all x1, blocking collectives, body(): lax.all_to_all(group_hidden, 'dp', split_axis=1, concat_axis=0, tiled=True)  56.6 us
    all_gather x3, blocking collectives, gathered_once(): both, at, found = (lax.all_gather(jnp.concatenate(lines), axis), 0, {})  40.8 us
    unnamed x1, blocking collectives  15 us
    all_to_all x2, local copies, waits for them, and re-layouts, body(): lax.all_to_all(group_hidden, 'dp', split_axis=1, concat_axis=0, tiled=True)  14.5 us
    dot_general x1, matrix products, body(): jnp.dot(every_rows, lm_head, preferred_element_type=jnp.float32)  12.4 us
  transfers between devices with their start and end apart: 2, of which 2 were waited for; matrix products, arithmetic and copies ran while one was open for 0% of the time, Pallas kernels for 0%

commit v1 on v0

--- a/solution.py
+++ b/solution.py
@@ -49,7 +49,15 @@
     shard_vocab = lm_head.shape[1]
     vocab_offset = lax.axis_index(VOCAB) * shard_vocab
     group_hidden, group_targets = (
-        lax.all_gather(hidden, VOCAB, axis=0, tiled=True),
+        jnp.concatenate(
+            jax.lax.all_to_all(
+                jnp.stack([hidden for _ in range(jax.lax.psum(1, axis_name=VOCAB))], axis=0),
+                concat_axis=0,
+                axis_name=VOCAB,
+                split_axis=0,
+            ),
+            0,
+        ),
         lax.all_gather(targets, VOCAB, axis=0, tiled=True),
     )
     every_rows = lax.all_to_all(group_hidden, "dp", split_axis=1, concat_axis=0, tiled=True)

time: 331 us -> 420 us (1.27)
  blocking collectives: 112 us -> 289 us
  waiting for transfers between devices: 166 us -> 77.6 us
    all_to_all x0 -> x1, blocking collectives: none -> 176 us  [body(): jax.lax.all_to_all(jnp.stack([hidden for _ in range(jax.lax.psum(1, axis_...]
    all_gather x1 -> x0, waiting for transfers between devices: 87.9 us -> none  [body(): lax.all_gather(hidden, VOCAB, axis=0, tiled=True)]
  transfers between devices with their start and end apart: 2 -> 1, of which waited for: 2 -> 1; matrix products, arithmetic and copies ran while one was open for 0% -> 0% of each run, Pallas kernels for 0% -> 0%
where the time goes in v1:
time: 420 us; the launch traced here: 419 us
  blocking collectives  289 us (69%)
  waiting for transfers between devices  77.6 us (18%)
  between operations  17.9 us (4%)
  local copies, waits for them, and re-layouts  16.6 us (4%)
  matrix products  12.4 us (3%)
  other arithmetic  5.75 us (1%)
    all_to_all x1, blocking collectives, body(): jax.lax.all_to_all(jnp.stack([hidden for _ in range(jax.lax.psum(1, axis_...  176 us
    reduce_scatter x1, waiting for transfers between devices, body(): lax.psum_scatter(jnp.dot(every_rows, lm_head, preferred_element_type=jnp....  77.6 us
    all_to_all x1, blocking collectives, body(): lax.all_to_all(group_hidden, 'dp', split_axis=1, concat_axis=0, tiled=True)  55.5 us
    all_gather x3, blocking collectives, gathered_once(): both, at, found = (lax.all_gather(jnp.concatenate(lines), axis), 0, {})  40.8 us
    unnamed x1, blocking collectives  16.5 us
    all_to_all x2, local copies, waits for them, and re-layouts, body(): lax.all_to_all(group_hidden, 'dp', split_axis=1, concat_axis=0, tiled=True)  14.5 us
    dot_general x1, matrix products, body(): jnp.dot(every_rows, lm_head, preferred_element_type=jnp.float32)  12.4 us
  transfers between devices with their start and end apart: 1, of which 1 were waited for; matrix products, arithmetic and copies ran while one was open for 0% of the time, Pallas kernels for 0%

profile of v1, /device:TPU:1, one launch (start us, length us, event | category | flops | bytes accessed | tf_op | source)
XLA Modules:
  0.0 419.2 jit_solution(12714442648289137944)
XLA Ops:
  7.2 0.0 reduce-scatter.2.cloned.1.call-start
  7.2 0.9 pad_maximum_fusion
  8.1 0.9 stack.2
  9.0 176.1 %all_to_all.24 = bf16[64,5,7168]{2,1,0:T(8,128)(2,1)} all-to-all(bf16[64,5,7168]{2,1,0:T(8,128)(2,1)S(1)} %stack.2), channel_id=1, replica_groups=mesh['dp'=4,'vocab_0'=8,'vocab_1'=4,'vocab_2'=2] {'vocab_0','vocab_1','v..., dimensions={0} | all-to-all | bytes 9175040 | tf_op jit(solution)/shard_map/all_to_all | solution.py:53
  185.1 11.4 %all_to_all.18 = bf16[320,4,1792]{2,1,0:T(4,128)(2,1)} reshape(bf16[64,5,7168]{2,1,0:T(8,128)(2,1)} %all_to_all.24) | data formatting | bytes 9175040 | tf_op jit(solution)/shard_map/all_to_all | solution.py:63
  196.5 0.0 slice-start
  196.5 3.0 copy.9
  199.5 0.0 slice-start.1
  199.6 55.5 %all_to_all.25 = bf16[320,4,1792]{2,0,1:T(8,128)(2,1)S(1)} all-to-all(bf16[320,4,1792]{2,0,1:T(8,128)(2,1)S(1)} %copy.9), channel_id=1, replica_groups=mesh['dp'=4,'vocab_0'=8,'vocab_1'=4,'vocab_2'=2] {'dp'}, dimensions={1} | all-to-all | bytes 9175040 | tf_op jit(solution)/shard_map/all_to_all | solution.py:63
  255.1 0.0 slice-done
  255.1 0.0 slice-done.1
  255.1 12.4 %fusion.47 = f32[1280,2020]{1,0:T(8,128)} fusion(bf16[1280,1792]{1,0:T(8,128)(2,1)S(1)} %bitcast.246, bf16[1792,2020]{0,1:T(8,128)(2,1)S(1)} %bitcast.248), kind=kOutput, calls=%fused_computation.95 | convolution fusion | flops 9266790400 | bytes 22169600 | tf_op jit(solution)/shard_map/dot_general | solution.py:65
  267.5 0.0 copy-start.1
  267.5 0.0 copy-start
  267.5 0.0 reduce-scatter.2.cloned.1.call-update
  268.8 0.0 copy-done.1
  268.9 0.6 dynamic-slice
  270.1 0.0 copy-done
  270.1 0.2 add_dynamic-update-slice_fusion
  270.3 16.5 %all-reduce = s32[320]{0:T(512)S(1)} all-reduce(s32[320]{0:T(512)S(1)} %add_dynamic-update-slice_fusion), channel_id=1, replica_groups=mesh['dp'=4,'vocab_0'=8,'vocab_1'=4,'vocab_2'=2] {'vocab_0','vocab_1','v..., use_global_device_ids=true, to_apply=%add | all-reduce | flops 320 | bytes 2560
  286.8 77.6 %reduce-scatter.2.cloned.1.call-done = f32[320,2020]{1,0:T(8,128)} async-done(((f32[1280,2020]{1,0:T(8,128)}), f32[320,2020]{1,0:T(8,128)}) %reduce-scatter.2.cloned.1.call-update) | async-done | bytes 2585616 | tf_op jit(solution)/shard_map/reduce_scatter | solution.py:64
  364.4 2.0 reduce_max.9
  366.4 2.5 exponential_reduce_fusion
  368.9 20.2 %all-gather.3 = f32[8,3,320]{2,1,0:T(4,128)S(1)} all-gather(f32[1,3,320]{2,1,0:T(4,128)S(1)} %maximum_bitcast_fusion), channel_id=2, replica_groups=mesh['dp'=4,'vocab_0'=8,'vocab_1'=4,'vocab_2'=2] {'vocab_0'}, dimensions={0}, use_global_device_ids=true | all-gather | bytes 34560 | tf_op jit(solution)/shard_map/all_gather | solution.py:19
  389.2 9.4 %all-gather.4 = f32[4,3,320]{2,1,0:T(4,128)S(1)} all-gather(f32[1,3,320]{2,1,0:T(4,128)S(1)} %maximum_bitcast_fusion.1), channel_id=3, replica_groups=mesh['dp'=4,'vocab_0'=8,'vocab_1'=4,'vocab_2'=2] {'vocab_1'}, dimensions={0}, use_global_device_ids=true | all-gather | bytes 19200 | tf_op jit(solution)/shard_map/all_gather | solution.py:19
  398.7 11.2 %all-gather.5 = f32[2,3,320]{2,1,0:T(4,128)S(1)} all-gather(f32[1,3,320]{2,1,0:T(4,128)S(1)} %maximum_bitcast_fusion.2), channel_id=4, replica_groups=mesh['dp'=4,'vocab_0'=8,'vocab_1'=4,'vocab_2'=2] {'vocab_2'}, dimensions={0}, use_global_device_ids=true | all-gather | bytes 11520 | tf_op jit(solution)/shard_map/all_gather | solution.py:19
  409.9 0.1 dynamic_slice.3
  410.0 0.0 copy-start.2
  410.0 0.6 slice.268
  411.2 0.0 copy-done.2
  (15 shorter events, 0.2 us)
Async XLA Ops:
  7.2 357.2 %reduce-scatter.2.cloned.1.call-start = ((), (), s32[]{:S(2)}) async-start(), calls=%async_computation.3 | async-start | bytes 13107200 | tf_op jit(solution)/shard_map/reduce_scatter | solution.py:64
  196.5 58.6 %slice-start = ((s8[7254016]{0:T(1024)(128)(4,1)}), s8[4194304]{0:T(1024)(128)(4,1)S(1)}, s32[]{:S(2)}) async-start(s8[7254016]{0:T(1024)(128)(4,1)} %bitcast.247), calls=%async_computation.4 | async-start | bytes 8388608
  199.5 55.5 %slice-start.1 = ((s8[7254016]{0:T(1024)(128)(4,1)}), s8[3059712]{0:T(1024)(128)(4,1)S(1)}, s32[]{:S(2)}) async-start(s8[7254016]{0:T(1024)(128)(4,1)} %bitcast.247), calls=%async_computation.5 | async-start | bytes 6119424
  267.5 1.3 copy-start.1
  267.5 2.6 copy-start
  410.0 1.2 copy-start.2
Sparse Core Ops, SparseCore 0:
  267.7 96.6 reduce-scatter.1
